TPU v7x, 32 devices: a whole 2x2x4 slice. The times are simulated.
32 devices in a mesh: blk: 16 (over z, y, core), head: 2 (over x).
Axes of the slice: x: 2, y: 2, z: 4, core: 2. Of those that a mesh axis runs over, the one named last changes fastest.
Arguments:
- queries: bfloat16 [8192, 16, 128], P('blk', 'head'), may hold values from -6 to 6
- out_grad: bfloat16 [8192, 16, 128], P('blk', 'head'), may hold values from -6 to 6
- outputs: bfloat16 [8192, 16, 128], P('blk', 'head'), may hold values from -6 to 6
- key_vectors: bfloat16 [8192, 128], P('blk'), may hold values from -6 to 6
- value_vectors: bfloat16 [8192, 128], P('blk'), may hold values from -6 to 6
- logsumexp: float32 [8192, 16], P('blk', 'head'), may hold values from 4 to 7
- positions: int32 [8192], P('blk'), may hold values from 0 to 8191, as said below
- doc_start: int32 [8192], P('blk'), may hold values from 0 to 8191, as said below
Outputs:
- query_grad: bfloat16 [8192, 16, 128], P('blk', 'head')
- key_grad: bfloat16 [8192, 128], P('blk')
- value_grad: bfloat16 [8192, 128], P('blk')
Inputs may be any that keep to these rules, and one draw needn't show every extreme that they name: positions is a permutation of 0 to 8191; row r holds position (r mod 512) * 16 + sigma(r div 512), sigma a permutation of the blocks of 512 rows. doc_start of a row is the first position of the document that holds the row's position; documents are runs of consecutive positions, the first starting at 0, and the last position starts a document of its own.
All inputs are finite; a program needn't handle non-finite values.
Results may differ from a plain program's by a relative error of at most 0.0063.
Values may be sent and summed in bfloat16 or wider, within the bound.
A program may use at most 64 MiB of HBM per device.

v0:
```python
import functools
import math

import jax
import jax.numpy as jnp
from jax import lax
from jax.experimental import pallas as pl
from jax.experimental.pallas import tpu as pltpu
from jax.sharding import PartitionSpec as P

STEPS = 4
TILE = 64
CHUNKS = 4
LOG2E = math.log2(math.e)
MESH = pl.DeviceIdType.MESH
VMEM_SPEC = pl.BlockSpec(memory_space=pltpu.VMEM)


def places(n):
    b = lax.axis_index("blk")
    h = lax.axis_index("head")
    even = lax.rem(b, 2) == 0
    partner = jnp.where(even, b + 1, b - 1)

    def at(d):
        return lax.rem(b + d + n, n)

    return b, h, even, partner, at


def greet(n):
    b, h, even, partner, at = places(n)
    barrier = pltpu.get_barrier_semaphore()
    for d in (-3, -2, -1, 1, 2, 3):
        pl.semaphore_signal(barrier, inc=1, device_id=(at(d), h), device_id_type=MESH)
    pl.semaphore_signal(barrier, inc=1, device_id=(b, 1 - h), device_id_type=MESH)
    pl.semaphore_wait(barrier, 7)


def gather_kernel(
    n, first_ref, k_ref, v_ref, lse_ref, start_ref, last_ref, g_hbm, o_hbm,
    kall, vall, pos_all, table, g_ref, o_ref, pos_ref, send, recv, local, wide,
):
    b, h, even, partner, at = places(n)
    rows = k_ref.shape[0]
    half = rows // 2
    mine = pl.ds(pl.multiple_of(h * half, half), half)
    other = pl.ds(pl.multiple_of((1 - h) * half, half), half)
    pairs = ((k_ref, kall), (v_ref, vall))

    def copy(src, dst, kind, j, who):
        return pltpu.make_async_remote_copy(
            src_ref=src,
            dst_ref=dst,
            send_sem=send.at[kind, j],
            recv_sem=recv.at[kind, j],
            device_id=who,
            device_id_type=MESH,
        )

    own = [
        pltpu.make_async_copy(src, dst.at[0], local.at[j])
        for j, (src, dst) in enumerate(pairs)
    ]
    wides = [
        pltpu.make_async_copy(src, dst, wide.at[j])
        for j, (src, dst) in enumerate(((g_hbm, g_ref), (o_hbm, o_ref)))
    ]
    pos_ref[...] = jnp.full(pos_ref.shape, first_ref[0], pos_ref.dtype)
    pos_all[0] = jnp.full(pos_ref.shape, first_ref[0], pos_ref.dtype)
    for c in own + wides:
        c.start()
    greet(n)
    pslot = jnp.where(even, 1, 3)
    qslot = jnp.where(even, 3, 1)
    first, third, near = [], [], []
    for j, (src, dst) in enumerate(pairs):
        first.append(copy(src.at[mine], dst.at[2, mine], 0, j, (at(-2), h)))
        third.append(copy(src.at[mine], dst.at[3, mine], 1, j, (at(-3), h)))
        near.append(copy(src, dst.at[1], 2, j, (partner, h)))
    for j in range(2):
        first[j].start()

        @pl.when(even)
        def _():
            third[j].start()

        @pl.when(jnp.logical_not(even))
        def _():
            near[j].start()

    marks = [
        copy(pos_ref, pos_all.at[d], 7 + d // 3, d % 3, (at(-d), h)) for d in range(1, STEPS)
    ]
    for c in marks:
        c.start()

    for c in wides:
        c.wait()
    heads, tokens = lse_ref.shape
    block = TILE * heads
    spread = (
        lax.broadcasted_iota(jnp.int32, (TILE, block), 1) // heads
        == lax.broadcasted_iota(jnp.int32, (TILE, block), 0)
    ).astype(jnp.bfloat16)
    choose = (
        lax.broadcasted_iota(jnp.int32, (heads, block), 1) % heads
        == lax.broadcasted_iota(jnp.int32, (heads, block), 0)
    )

    def spread_whole(values):
        upper = values // 256
        lower = values - upper * 256
        up, low = (
            jnp.dot(
                jnp.broadcast_to(part.astype(jnp.float32), (8, TILE)).astype(jnp.bfloat16),
                spread,
                preferred_element_type=jnp.float32,
            )
            for part in (upper, lower)
        )
        return (up * 256.0 + low)[0:1]

    ones = jnp.ones((8, g_ref.shape[1]), jnp.bfloat16)
    contract = (((1,), (1,)), ((), ()))
    for c in range(g_ref.shape[0] // block):
        r = pl.ds(c * block, block)
        product = g_ref[r].astype(jnp.float32) * o_ref[r].astype(jnp.float32)
        upper = product.astype(jnp.bfloat16)
        lower = (product - upper.astype(jnp.float32)).astype(jnp.bfloat16)
        delta = lax.dot_general(
            ones, upper, contract, preferred_element_type=jnp.float32
        ) + lax.dot_general(ones, lower, contract, preferred_element_type=jnp.float32)
        table[0:1, r] = delta[0:1]
        rest = lse_ref[:, c * TILE : (c + 1) * TILE] * LOG2E
        lse = jnp.zeros((heads, block), jnp.float32)
        for _ in range(3):
            part = rest.astype(jnp.bfloat16)
            rest = rest - part.astype(jnp.float32)
            lse += jnp.dot(part, spread, preferred_element_type=jnp.float32)
        table[1:2, r] = jnp.sum(jnp.where(choose, lse, 0.0), axis=0, keepdims=True)
        at = slice(c * TILE, (c + 1) * TILE)
        table[2:3, r] = spread_whole(start_ref[:, at])
        table[3:4, r] = spread_whole(last_ref[:, at])

    side, side3, fwd, fwd2 = [], [], [], []
    for j, (src, dst) in enumerate(pairs):
        side.append(copy(dst.at[2, mine], dst.at[2, mine], 3, j, (b, 1 - h)))
        side3.append(copy(dst.at[3, mine], dst.at[3, mine], 4, j, (b, 1 - h)))
        fwd.append(copy(dst.at[2, mine], dst.at[pslot, mine], 5, j, (partner, h)))
        fwd2.append(copy(dst.at[2, other], dst.at[pslot, other], 6, j, (partner, h)))
    for j in range(2):
        first[j].wait_recv()
        side[j].start()
        fwd[j].start()
    for j in range(2):

        @pl.when(jnp.logical_not(even))
        def _():
            third[j].wait_recv()
            side3[j].start()

    for j in range(2):
        side[j].wait_recv()
        fwd2[j].start()
    for j in range(2):
        fwd[j].wait_recv()
        fwd2[j].wait_recv()

        @pl.when(even)
        def _():
            near[j].wait_recv()
            third[j].wait_send()

        @pl.when(jnp.logical_not(even))
        def _():
            side3[j].wait_recv()
            near[j].wait_send()
            side3[j].wait_send()

        first[j].wait_send()
        side[j].wait_send()
        fwd[j].wait_send()
        fwd2[j].wait_send()
    for c in own + marks:
        c.wait()


def gather(n, keys, values, logsumexp, positions, doc_start, g, o):
    rows, width = keys.shape
    shape = jax.ShapeDtypeStruct((STEPS, rows, width), keys.dtype)
    mark = (8, width)
    return pl.pallas_call(
        functools.partial(gather_kernel, n),
        out_shape=(
            shape,
            shape,
            jax.ShapeDtypeStruct((STEPS,) + mark, positions.dtype),
            jax.ShapeDtypeStruct((4, g.shape[0]), jnp.float32),
        ),
        in_specs=[pl.BlockSpec(memory_space=pltpu.SMEM)]
        + [VMEM_SPEC] * 5
        + [pl.BlockSpec(memory_space=pltpu.HBM)] * 2,
        out_specs=(VMEM_SPEC,) * 4,
        scratch_shapes=[
            pltpu.VMEM(g.shape, g.dtype),
            pltpu.VMEM(g.shape, g.dtype),
            pltpu.VMEM(mark, positions.dtype),
            pltpu.SemaphoreType.DMA((9, 3)),
            pltpu.SemaphoreType.DMA((9, 3)),
            pltpu.SemaphoreType.DMA((2,)),
            pltpu.SemaphoreType.DMA((2,)),
        ],
        compiler_params=pltpu.CompilerParams(
            collective_id=0, has_side_effects=True, vmem_limit_bytes=16 << 20
        ),
        cost_estimate=pl.CostEstimate(
            flops=32 * g.size, bytes_accessed=16 * g.size, transcendentals=0
        ),
        name="gather_kv",
    )(
        positions,
        keys,
        values,
        logsumexp.T,
        doc_start.reshape(1, -1),
        positions.reshape(1, -1),
        g,
        o,
    )


def compute_kernel(
    n, tile, start_ref, q_ref, g_ref, table, k_ref, v_ref, marks_ref,
    dq_ref, dk_ref, dv_ref, dk_acc, dv_acc, dq_acc, p_buf, ds_buf, kp_buf,
):
    steps, tokens, width = k_ref.shape
    count = tokens // tile
    block = q_ref.shape[0] // count
    keys = steps * tile
    scaling = width ** (-0.5)
    contract = (((1,), (1,)), ((), ()))

    dk_acc[...] = jnp.zeros_like(dk_acc)
    dv_acc[...] = jnp.zeros_like(dv_acc)
    dq_acc[...] = jnp.zeros_like(dq_acc)
    ramp = lax.broadcasted_iota(jnp.int32, (tile, width), 0) * n
    for s in range(steps):
        kp_buf[s * tile : (s + 1) * tile, :] = (
            ramp + marks_ref[s, 0:1, :]
        ).astype(jnp.float32)

    def lowest(i):
        return start_ref[i * tile] // (n * tile)

    def probs(i, t):
        at = pl.ds(pl.multiple_of(t * tile, tile), tile)
        r = pl.ds(pl.multiple_of(i * block, block), block)
        k = k_ref[:, at, :].reshape(keys, width)
        v = v_ref[:, at, :].reshape(keys, width)
        moved = (t * (tile * n)).astype(jnp.float32)
        start = table[2:3, r] - moved
        last = table[3:4, r] - moved
        kp = jnp.concatenate([kp_buf[...]] * (block // width), axis=1)
        s = lax.dot_general(k, q_ref[r, :], contract, preferred_element_type=jnp.float32)
        dp = lax.dot_general(v, g_ref[r, :], contract, preferred_element_type=jnp.float32)
        ok = (kp <= last) & (kp >= start)
        p = jnp.where(ok, jnp.exp2(s * (scaling * LOG2E) - table[1:2, r]), 0.0)
        return p.astype(jnp.bfloat16), (p * (dp - table[0:1, r])).astype(jnp.bfloat16)

    def add_grads(i, t):
        at = pl.ds(pl.multiple_of(t * tile, tile), tile)
        r = pl.ds(pl.multiple_of(i * block, block), block)
        k = k_ref[:, at, :].reshape(keys, width)
        ds = ds_buf[...]
        dv = jnp.dot(p_buf[...], g_ref[r, :], preferred_element_type=jnp.float32)
        dk = jnp.dot(ds, q_ref[r, :], preferred_element_type=jnp.float32)
        dv_acc[:, at, :] += dv.reshape(steps, tile, width)
        dk_acc[:, at, :] += dk.reshape(steps, tile, width)
        dq_acc[r, :] += lax.dot_general(
            ds, k, (((0,), (0,)), ((), ())), preferred_element_type=jnp.float32
        )

    def put(pair):
        p_buf[...], ds_buf[...] = pair

    total = lax.fori_loop(0, count, lambda i, c: c + i - lowest(i) + 1, 0)
    put(probs(0, lowest(0)))

    def body(_, spot):
        i, t = spot
        done = t >= i
        new_i = jnp.where(done, i + 1, i)
        new_t = jnp.where(done, lowest(new_i), t + 1)
        pair = probs(new_i, new_t)
        add_grads(i, t)
        put(pair)
        return new_i, new_t

    i, t = lax.fori_loop(1, total, body, (jnp.int32(0), lowest(0)))
    add_grads(i, t)
    dq_ref[...] = (dq_acc[...] * scaling).astype(dq_ref.dtype)
    dk_ref[...] = (dk_acc[...] * scaling).astype(dk_ref.dtype)
    dv_ref[...] = dv_acc[...].astype(dv_ref.dtype)


def compute(n, tile, starts, q, g, table, kall, vall, marks):
    steps, tokens, width = kall.shape
    block = q.shape[0] // (tokens // tile)
    part = jax.ShapeDtypeStruct(kall.shape, jnp.bfloat16)
    return pl.pallas_call(
        functools.partial(compute_kernel, n, tile),
        out_shape=(jax.ShapeDtypeStruct(q.shape, q.dtype), part, part),
        in_specs=[pl.BlockSpec(memory_space=pltpu.SMEM)] + [VMEM_SPEC] * 6,
        out_specs=(VMEM_SPEC,) * 3,
        scratch_shapes=[
            pltpu.VMEM(kall.shape, jnp.float32),
            pltpu.VMEM(kall.shape, jnp.float32),
            pltpu.VMEM(q.shape, jnp.float32),
            pltpu.VMEM((steps * tile, block), jnp.bfloat16),
            pltpu.VMEM((steps * tile, block), jnp.bfloat16),
            pltpu.VMEM((steps * tile, width), jnp.float32),
        ],
        compiler_params=pltpu.CompilerParams(vmem_limit_bytes=28 << 20),
        cost_estimate=pl.CostEstimate(
            flops=10 * q.shape[0] * steps * tokens * width // 2,
            bytes_accessed=6 * q.size,
            transcendentals=q.shape[0] * steps * tokens // 2,
        ),
        name="block_grads",
    )(starts, q, g, table, kall, vall, marks)


def reduce_kernel(
    n, pk, pv, total_k, total_v, last_k, last_v, near, both, far, mid, guest, send, recv
):
    b, h, even, partner, at = places(n)
    rows = pk.shape[1]
    size = rows // CHUNKS
    parts = (pk, pv)
    total = (total_k, total_v)
    last = (last_k, last_v)
    odd = jnp.logical_not(even)

    def copy(src, dst, kind, j, c, who):
        return pltpu.make_async_remote_copy(
            src_ref=src,
            dst_ref=dst,
            send_sem=send.at[kind, j, c],
            recv_sem=recv.at[kind, j, c],
            device_id=who,
            device_id_type=MESH,
        )

    greet(n)
    work = [(j, c, pl.ds(c * size, size)) for c in range(CHUNKS) for j in range(2)]
    give, own, skip, hop, side = {}, {}, {}, {}, {}
    gslot = jnp.where(even, 3, 1)
    for j, c, r in work:
        give[j, c] = copy(parts[j].at[gslot, r], near.at[j, r], 0, j, c, (partner, h))
        own[j, c] = copy(parts[j].at[1, r], both.at[j, r], 1, j, c, (partner, h))
        skip[j, c] = copy(parts[j].at[3, r], far.at[j, r], 2, j, c, (at(3), h))
        hop[j, c] = copy(mid.at[j, r], guest.at[j, r], 3, j, c, (at(2), h))
        side[j, c] = copy(total[j].at[r], last[j].at[r], 4, j, c, (b, 1 - h))
        give[j, c].start()
    for j, c, r in work:
        give[j, c].wait_recv()
        mid[j, r] = (parts[j][2, r].astype(jnp.float32) + near[j, r].astype(jnp.float32)).astype(mid.dtype)
        hop[j, c].start()

        @pl.when(odd)
        def _():
            skip[j, c].start()

        @pl.when(even)
        def _():
            own[j, c].start()

    for j, c, r in work:
        hop[j, c].wait_recv()
        acc = parts[j][0, r].astype(jnp.float32) + guest[j, r].astype(jnp.float32)

        @pl.when(even)
        def _():
            skip[j, c].wait_recv()
            total[j][r] = (acc + far[j, r].astype(jnp.float32)).astype(mid.dtype)

        @pl.when(odd)
        def _():
            own[j, c].wait_recv()
            total[j][r] = (acc + both[j, r].astype(jnp.float32)).astype(mid.dtype)

        side[j, c].start()
    for j, c, r in work:
        side[j, c].wait_recv()
    for j, c, r in work:
        give[j, c].wait_send()
        hop[j, c].wait_send()
        side[j, c].wait_send()

        @pl.when(odd)
        def _():
            skip[j, c].wait_send()

        @pl.when(even)
        def _():
            own[j, c].wait_send()


def reduce_parts(n, pk, pv):
    steps, rows, width = pk.shape
    out = jax.ShapeDtypeStruct((rows, width), jnp.bfloat16)
    buf = pltpu.VMEM((2, rows, width), jnp.bfloat16)
    return pl.pallas_call(
        functools.partial(reduce_kernel, n),
        out_shape=(out,) * 4,
        in_specs=[VMEM_SPEC] * 2,
        out_specs=(VMEM_SPEC,) * 4,
        scratch_shapes=[
            buf,
            buf,
            buf,
            buf,
            buf,
            pltpu.SemaphoreType.DMA((5, 2, CHUNKS)),
            pltpu.SemaphoreType.DMA((5, 2, CHUNKS)),
        ],
        compiler_params=pltpu.CompilerParams(
            collective_id=1, has_side_effects=True, vmem_limit_bytes=12 << 20
        ),
        name="reduce_parts",
    )(pk, pv)


def on_device(
    n, queries, out_grad, outputs, key_vectors, value_vectors, logsumexp, positions, doc_start
):
    tokens, heads, width = queries.shape
    q = queries.reshape(-1, width)
    g = out_grad.reshape(-1, width)
    kall, vall, marks, table = gather(
        n, key_vectors, value_vectors, logsumexp, positions, doc_start, g, outputs.reshape(-1, width)
    )
    dq, pk, pv = compute(n, TILE, doc_start, q, g, table, kall, vall, marks)
    total_k, total_v, last_k, last_v = reduce_parts(n, pk, pv)
    dk = (total_k.astype(jnp.float32) + last_k.astype(jnp.float32)).astype(jnp.bfloat16)
    dv = (total_v.astype(jnp.float32) + last_v.astype(jnp.float32)).astype(jnp.bfloat16)
    return dq.reshape(queries.shape), dk, dv


def solution(mesh):
    n = mesh.shape["blk"]
    in_specs = (
        P("blk", "head", None),
        P("blk", "head", None),
        P("blk", "head", None),
        P("blk", None),
        P("blk", None),
        P("blk", "head"),
        P("blk"),
        P("blk"),
    )
    out_specs = (P("blk", "head", None), P("blk", None), P("blk", None))
    return jax.shard_map(
        functools.partial(on_device, n),
        mesh=mesh,
        in_specs=in_specs,
        out_specs=out_specs,
        check_vma=False,
    )
```

profile of v0, /device:TPU:1, one launch (start us, length us, event | category | flops | bytes accessed | tf_op | source)
XLA Modules:
  0.0 53.4 jit_solution(7059831179895161704)
XLA Ops:
  0.6 0.0 copy-start.7
  0.6 0.0 copy-start.6
  0.7 0.7 %copy-done.7 = s32[512]{0:T(512)S(1)} copy-done((s32[512]{0:T(512)S(1)}, s32[512]{0:T(512)}, u32[]{:S(2)}) %copy-start.7) | copy-done | bytes 2072
  1.3 0.0 copy-done.6
  1.3 0.0 copy-start
  1.3 1.2 %copy-done = bf16[512,8,128]{2,1,0:T(8,128)(2,1)S(1)} copy-done((bf16[512,8,128]{2,1,0:T(8,128)(2,1)S(1)}, bf16[512,8,128]{2,1,0:T(8,128)(2,1)}, u32[]{:S(2)}) %copy-start) | copy-done | bytes 1048600
  2.6 0.0 copy-start.1
  2.6 1.2 %copy-done.1 = bf16[512,8,128]{2,1,0:T(8,128)(2,1)S(1)} copy-done((bf16[512,8,128]{2,1,0:T(8,128)(2,1)S(1)}, bf16[512,8,128]{2,1,0:T(8,128)(2,1)}, u32[]{:S(2)}) %copy-start.1) | copy-done | bytes 1048600
  3.8 0.0 copy-start.3
  3.8 0.9 %copy-done.3 = bf16[512,128]{1,0:T(8,128)(2,1)S(1)} copy-done((bf16[512,128]{1,0:T(8,128)(2,1)S(1)}, bf16[512,128]{1,0:T(8,128)(2,1)}, u32[]{:S(2)}) %copy-start.3) | copy-done | bytes 131096
  4.7 0.0 copy-start.4
  4.7 0.9 %copy-done.4 = bf16[512,128]{1,0:T(8,128)(2,1)S(1)} copy-done((bf16[512,128]{1,0:T(8,128)(2,1)S(1)}, bf16[512,128]{1,0:T(8,128)(2,1)}, u32[]{:S(2)}) %copy-start.4) | copy-done | bytes 131096
  5.6 0.0 copy-start.5
  5.6 0.7 %copy-done.5 = f32[512,8]{0,1:T(8,128)S(1)} copy-done((f32[512,8]{0,1:T(8,128)S(1)}, f32[512,8]{0,1:T(8,128)}, u32[]{:S(2)}) %copy-start.5) | copy-done | bytes 16408
  6.3 0.0 copy-start.2
  6.3 0.0 copy-start.8
  6.3 16.4 %gather_kv.1 = (bf16[4,512,128]{2,1,0:T(8,128)(2,1)S(1)}, bf16[4,512,128]{2,1,0:T(8,128)(2,1)S(1)}, s32[4,8,128]{2,1,0:T(8,128)S(1)}, f32[4,4096]{1,0:T(4,128)S(1)}) custom-call(s32[512]{0:T(512)S(1)} %copy-done.6, bf16[512,128]{1,0:T(8,128)(2,1)S(1)} %copy-done.3, bf16[512,128]{1,0:T(8,128)(2,1)S(1)} %copy-done.4, f32[8,512]{1,0:T(8,128)S(1)} %bitcast.10, ...), custom_call_target="tpu_custom_call" | custom-call | flops 16777216 | bytes 8388608 | tf_op jit(solution)/shard_map/gather_kv/pallas_call | solution.py:193
  22.7 0.0 copy-done.2
  22.7 0.0 copy-done.8
  22.7 10.8 %block_grads.1 = (bf16[4096,128]{1,0:T(8,128)(2,1)}, bf16[4,512,128]{2,1,0:T(8,128)(2,1)S(1)}, bf16[4,512,128]{2,1,0:T(8,128)(2,1)S(1)}) custom-call(s32[512]{0:T(512)S(1)} %copy-done.7, bf16[4096,128]{1,0:T(8,128)(2,1)S(1)} %bitcast.13, bf16[4096,128]{1,0:T(8,128)(2,1)S(1)} %bitcast.9, f32[4,4096]{1,0:T(4,128)S(1)} %get-tuple-element.14.table, ...), custom_call_target="tpu_custom_call" | custom-call | flops 5368709120 | bytes 3145728 | tf_op jit(solution)/shard_map/block_grads/pallas_call | solution.py:311
  33.5 19.1 %reduce_parts.1 = (bf16[512,128]{1,0:T(8,128)(2,1)S(1)}, bf16[512,128]{1,0:T(8,128)(2,1)S(1)}, bf16[512,128]{1,0:T(8,128)(2,1)S(1)}, bf16[512,128]{1,0:T(8,128)(2,1)S(1)}) custom-call(bf16[4,512,128]{2,1,0:T(8,128)(2,1)S(1)} %get-tuple-element.19.pk, bf16[4,512,128]{2,1,0:T(8,128)(2,1)S(1)} %get-tuple-element.20.pv), custom_call_target="tpu_custom_call" | custom-call | tf_op jit(solution)/shard_map/reduce_parts/pallas_call | solution.py:414
  52.7 0.8 %add_convert_fusion = (bf16[512,128]{1,0:T(8,128)(2,1)}, bf16[512,128]{1,0:T(8,128)(2,1)}) fusion(bf16[512,128]{1,0:T(8,128)(2,1)S(1)} %get-tuple-element.24, bf16[512,128]{1,0:T(8,128)(2,1)S(1)} %get-tuple-element.23, bf16[512,128]{1,0:T(8,128)(2,1)S(1)} %get-tuple-element.22, bf16[512,128]{1,0:T(8,128)(2,1)S(1)} %get-tuple-element.21), kind=kLoop, calls=%fused_computation | loop fusion | flops 524288 | bytes 786432 | tf_op jit(solution)/shard_map/convert_element_type | solution.py:447
Async XLA Ops:
  0.6 0.7 %copy-start.7 = (s32[512]{0:T(512)S(1)}, s32[512]{0:T(512)}, u32[]{:S(2)}) copy-start(s32[512]{0:T(512)} %start_ref.1) | copy-start | bytes 6148
  0.6 0.7 %copy-start.6 = (s32[512]{0:T(512)S(1)}, s32[512]{0:T(512)}, u32[]{:S(2)}) copy-start(s32[512]{0:T(512)} %first_ref.1) | copy-start | bytes 6148
  1.3 1.2 %copy-start = (bf16[512,8,128]{2,1,0:T(8,128)(2,1)S(1)}, bf16[512,8,128]{2,1,0:T(8,128)(2,1)}, u32[]{:S(2)}) copy-start(bf16[512,8,128]{2,1,0:T(8,128)(2,1)} %param.10) | copy-start | bytes 3145732
  2.6 1.2 %copy-start.1 = (bf16[512,8,128]{2,1,0:T(8,128)(2,1)S(1)}, bf16[512,8,128]{2,1,0:T(8,128)(2,1)}, u32[]{:S(2)}) copy-start(bf16[512,8,128]{2,1,0:T(8,128)(2,1)} %param.9) | copy-start | bytes 3145732
  3.8 0.9 %copy-start.3 = (bf16[512,128]{1,0:T(8,128)(2,1)S(1)}, bf16[512,128]{1,0:T(8,128)(2,1)}, u32[]{:S(2)}) copy-start(bf16[512,128]{1,0:T(8,128)(2,1)} %k_ref.1) | copy-start | bytes 393220
  4.7 0.9 %copy-start.4 = (bf16[512,128]{1,0:T(8,128)(2,1)S(1)}, bf16[512,128]{1,0:T(8,128)(2,1)}, u32[]{:S(2)}) copy-start(bf16[512,128]{1,0:T(8,128)(2,1)} %v_ref.1) | copy-start | bytes 393220
  5.6 0.7 %copy-start.5 = (f32[512,8]{0,1:T(8,128)S(1)}, f32[512,8]{0,1:T(8,128)}, u32[]{:S(2)}) copy-start(f32[512,8]{0,1:T(8,128)} %param.13) | copy-start | bytes 49156
  6.3 16.4 %copy-start.2 = (bf16[512,8,128]{2,1,0:T(8,128)(2,1)S(1)}, bf16[512,8,128]{2,1,0:T(8,128)(2,1)}, u32[]{:S(2)}) copy-start(bf16[512,8,128]{2,1,0:T(8,128)(2,1)} %param.9) | copy-start | bytes 3145732
  6.3 16.4 %copy-start.8 = (bf16[512,8,128]{2,1,0:T(8,128)(2,1)S(1)}, bf16[512,8,128]{2,1,0:T(8,128)(2,1)}, u32[]{:S(2)}) copy-start(bf16[512,8,128]{2,1,0:T(8,128)(2,1)} %param.8) | copy-start | bytes 3145732
where the time goes:
time: 54 us; the launch traced here: 53.4 us
  Pallas kernels  46.3 us (86%)
  local copies, waits for them, and re-layouts  5.66 us (10%)
  other arithmetic  0.77 us (1%)
  between operations  0.69 us (1%)
    pallas_call x1, Pallas kernels, reduce_parts(): pl.pallas_call(functools.partial(reduce_kernel, n), out_shape=(out,) * 4,...  19.1 us
    pallas_call x1, Pallas kernels, gather(): pl.pallas_call(functools.partial(gather_kernel, n), out_shape=(shape, sha...  16.4 us
    pallas_call x1, Pallas kernels, compute(): pl.pallas_call(functools.partial(compute_kernel, n, tile), out_shape=(jax...  10.8 us
    unnamed x18, local copies, waits for them, and re-layouts  5.66 us

commit v1 on v0

--- a/solution.py
+++ b/solution.py
@@ -212,7 +212,7 @@
             pltpu.SemaphoreType.DMA((2,)),
         ],
         compiler_params=pltpu.CompilerParams(
-            collective_id=0, has_side_effects=True, vmem_limit_bytes=16 << 20
+            collective_id=0, has_side_effects=True
         ),
         cost_estimate=pl.CostEstimate(
             flops=32 * g.size, bytes_accessed=16 * g.size, transcendentals=0
@@ -321,7 +321,7 @@
             pltpu.VMEM((steps * tile, block), jnp.bfloat16),
             pltpu.VMEM((steps * tile, width), jnp.float32),
         ],
-        compiler_params=pltpu.CompilerParams(vmem_limit_bytes=28 << 20),
+        compiler_params=pltpu.CompilerParams(),
         cost_estimate=pl.CostEstimate(
             flops=10 * q.shape[0] * steps * tokens * width // 2,
             bytes_accessed=6 * q.size,
@@ -426,7 +426,7 @@
             pltpu.SemaphoreType.DMA((5, 2, CHUNKS)),
         ],
         compiler_params=pltpu.CompilerParams(
-            collective_id=1, has_side_effects=True, vmem_limit_bytes=12 << 20
+            collective_id=1, has_side_effects=True
         ),
         name="reduce_parts",
     )(pk, pv)

time: 54 us -> 54.3 us (level); the launches traced: 53.4 us -> 54.7 us
  Pallas kernels: 46.3 us -> 52.1 us
  local copies, waits for them, and re-layouts: 5.66 us -> 0 us
  other arithmetic: 0.77 us -> 1.86 us
    unnamed x18 -> x0, local copies, waits for them, and re-layouts: 5.66 us -> none
    pallas_call x1, Pallas kernels: 10.8 us -> 13.3 us  [compute(): pl.pallas_call(functools.partial(compute_kernel, n, tile), out_shape=(jax...]
    pallas_call x1, Pallas kernels: 19.1 us -> 21.2 us  [reduce_parts(): pl.pallas_call(functools.partial(reduce_kernel, n), out_shape=(out,) * 4,...]
    pallas_call x1, Pallas kernels: 16.4 us -> 17.7 us  [gather(): pl.pallas_call(functools.partial(gather_kernel, n), out_shape=(shape, sha...]
    convert_element_type x1, other arithmetic: 0.77 us -> 1.86 us  [on_device(): (total_v.astype(jnp.float32) + last_v.astype(jnp.float32)).astype(jnp.bfl...]
where the time goes in v1:
time: 54.3 us; the launch traced here: 54.7 us
  Pallas kernels  52.1 us (96%)
  other arithmetic  1.86 us (3%)
  between operations  0.65 us (1%)
    pallas_call x1, Pallas kernels, reduce_parts(): pl.pallas_call(functools.partial(reduce_kernel, n), out_shape=(out,) * 4,...  21.2 us
    pallas_call x1, Pallas kernels, gather(): pl.pallas_call(functools.partial(gather_kernel, n), out_shape=(shape, sha...  17.7 us
    pallas_call x1, Pallas kernels, compute(): pl.pallas_call(functools.partial(compute_kernel, n, tile), out_shape=(jax...  13.3 us
    convert_element_type x1, other arithmetic, on_device(): (total_v.astype(jnp.float32) + last_v.astype(jnp.float32)).astype(jnp.bfl...  1.86 us

profile of v1, /device:TPU:1, one launch (start us, length us, event | category | flops | bytes accessed | tf_op | source)
XLA Modules:
  0.0 54.7 jit_solution(2890686900349301703)
XLA Ops:
  0.6 17.7 %gather_kv.1 = (bf16[4,512,128]{2,1,0:T(8,128)(2,1)}, bf16[4,512,128]{2,1,0:T(8,128)(2,1)}, s32[4,8,128]{2,1,0:T(8,128)}, f32[4,4096]{1,0:T(4,128)}) custom-call(s32[512]{0:T(512)} %first_ref.1, bf16[512,128]{1,0:T(8,128)(2,1)} %k_ref.1, bf16[512,128]{1,0:T(8,128)(2,1)} %v_ref.1, f32[8,512]{1,0:T(8,128)} %bitcast.10, s32[1,512]{1,0:T(1,128)} %bitcast.12, ...), custom_call_target="tpu_custom_call" | custom-call | flops 16777216 | bytes 8388608 | tf_op jit(solution)/shard_map/gather_kv/pallas_call | solution.py:193
  18.3 13.3 %block_grads.1 = (bf16[4096,128]{1,0:T(8,128)(2,1)}, bf16[4,512,128]{2,1,0:T(8,128)(2,1)}, bf16[4,512,128]{2,1,0:T(8,128)(2,1)}) custom-call(s32[512]{0:T(512)} %start_ref.1, bf16[4096,128]{1,0:T(8,128)(2,1)} %bitcast.13, bf16[4096,128]{1,0:T(8,128)(2,1)} %bitcast.9, f32[4,4096]{1,0:T(4,128)} %get-tuple-element.14.table, ...), custom_call_target="tpu_custom_call" | custom-call | flops 5368709120 | bytes 3145728 | tf_op jit(solution)/shard_map/block_grads/pallas_call | solution.py:311
  31.6 21.2 %reduce_parts.1 = (bf16[512,128]{1,0:T(8,128)(2,1)}, bf16[512,128]{1,0:T(8,128)(2,1)}, bf16[512,128]{1,0:T(8,128)(2,1)}, bf16[512,128]{1,0:T(8,128)(2,1)}) custom-call(bf16[4,512,128]{2,1,0:T(8,128)(2,1)} %get-tuple-element.19.pk, bf16[4,512,128]{2,1,0:T(8,128)(2,1)} %get-tuple-element.20.pv), custom_call_target="tpu_custom_call" | custom-call | tf_op jit(solution)/shard_map/reduce_parts/pallas_call | solution.py:414
  52.8 1.9 %add_convert_fusion = (bf16[512,128]{1,0:T(8,128)(2,1)}, bf16[512,128]{1,0:T(8,128)(2,1)}) fusion(bf16[512,128]{1,0:T(8,128)(2,1)} %get-tuple-element.24, bf16[512,128]{1,0:T(8,128)(2,1)} %get-tuple-element.23, bf16[512,128]{1,0:T(8,128)(2,1)} %get-tuple-element.22, bf16[512,128]{1,0:T(8,128)(2,1)} %get-tuple-element.21), kind=kLoop, calls=%fused_computation | loop fusion | flops 524288 | bytes 786432 | tf_op jit(solution)/shard_map/convert_element_type | solution.py:447
